TPU v7x, 512 devices: a whole 4x4x16 slice. The times are simulated.
512 devices in a mesh: obs: 16 (over x, y), patch: 32 (over z, core).
Axes of the slice: x: 4, y: 4, z: 16, core: 2. Of those that a mesh axis runs over, the one named last changes fastest.
Arguments:
- green: float32 [20480, 20480], P('obs', 'patch'), may hold values from -0.0390625 to 0.0390625
- data: float32 [20480, 128], P('obs'), may hold values from -6 to 6
- neighbours: int32 [3, 20480], P(None, 'patch'), may hold values from 0 to 20479, as said below
- reg_weight: float32 [128], replicated, may hold values from 0.5 to 2
Outputs:
- slip: float32 [20480, 128], P('patch')
Inputs may be any that keep to these rules, and one draw needn't show every extreme that they name: `neighbours`: entry (k, i) is a patch within 128 of i; an entry equal to i is padding. Distance 128 is reached in every draw.
All inputs are finite; a program needn't handle non-finite values.
Results may differ from a plain program's by a relative error of at most 0.0001.
Values sent between devices are 32-bit elements; how exact they have to be, the bound alone decides.
A program may use at most 64 MiB of HBM per device.

v0:
```python
import jax
import jax.numpy as jnp
from jax import lax
from jax.sharding import Mesh
from jax.sharding import PartitionSpec as P

BAND = 128
ITERS = 3
PATCH = ("patch_0", "patch_1")
OBS = ("obs_0", "obs_1")
OBS_PATCH = ("obs_0", "obs_1", "patch_0", "patch_1")


def extended_2(shard, sides, width):
    for axis, dim in sides:
        size, length = (lax.axis_size(axis), shard.shape[dim])
        up = [(i, (i + 1) % size) for i in range(size - 1)]
        down = [(j, i) for i, j in up]
        last = lax.slice_in_dim(shard, length - width, length, axis=dim)
        first = lax.slice_in_dim(shard, 0, width, axis=dim)
        before = lax.ppermute(last, axis, up)
        after = lax.ppermute(first, axis, down)
        shard = jnp.concatenate([before, shard, after], axis=dim)
    return shard


def shifted(value, axis, steps):
    count = lax.axis_size(axis)
    first, last = (max(0, -steps), min(count, count - steps))
    return lax.ppermute(value, axis, [(source, source + steps) for source in range(first, last)])


def cut_along(shard, dim, length):
    before, after = (shard.shape[:dim], shard.shape[dim + 1 :])
    return jnp.moveaxis(shard.reshape(*before, length, -1, *after), dim, 0)


def summed_on_arrival(shard, axis, dim):
    length = lax.axis_size(axis)
    pieces = lax.all_to_all(cut_along(shard, dim, length), axis, 0, 0, tiled=True)
    return jnp.sum(pieces, axis=0)


def joined_along(pieces, dim):
    dims = list(pieces.shape[1:])
    dims[dim] *= pieces.shape[0]
    return jnp.moveaxis(pieces, 0, dim).reshape(dims)


def all_blocks(shard, axes, sequence):
    pieces = shard[None]
    for k in sequence:
        pieces = lax.all_gather(pieces, axes[k], axis=0, tiled=True)
    block = [lax.axis_size(axes[k]) for k in reversed(sequence)]
    pieces = pieces.reshape(*block, *shard.shape)
    turned = sorted(range(len(sequence)), key=lambda place: sequence[len(sequence) - 1 - place])
    return pieces.transpose(*turned, *range(len(sequence), pieces.ndim)).reshape(-1, *shard.shape)


def gather_axes(shard, axes, sequence, dim):
    return joined_along(all_blocks(shard, axes, sequence), dim)


def total_of_pieces(shard, axis):
    pieces = lax.all_gather(shard, axis)
    return pieces.sum(axis=0)


def sent_to_all(shard, axis):
    length = lax.axis_size(axis)
    return lax.all_to_all(
        jnp.broadcast_to(shard[None], (length, *shard.shape)), axis, 0, 0, tiled=True
    )


def taken_together(shard, axis):
    everything = sent_to_all(shard, axis)
    return jnp.sum(everything, axis=0)


def over_axes_2(shard, axes):
    for axis in axes:
        shard = lax.psum(shard, axis)
    return shard


def back_product(block, residual):
    return lax.dot_general(
        block,
        residual,
        (((0,), (0,)), ((), ())),
        precision=lax.Precision.HIGHEST,
        preferred_element_type=jnp.float32,
    )


def shards(green, data, neighbours, reg_weight):
    highest = lax.Precision.HIGHEST
    row_count, col_count = green.shape
    epochs = data.shape[1]
    n_patch = lax.axis_size(PATCH)
    offset = lax.axis_index(PATCH) * col_count
    local_ids = neighbours - offset + BAND
    obs_first = lax.axis_index(OBS) == 0
    share = row_count // n_patch
    residual = lax.dynamic_slice_in_dim(data, lax.axis_index(PATCH) * share, share, 0)

    def back_partial(residual):
        return back_product(green, gather_axes(residual, PATCH, (0, 1), 0))

    def gradient_of(residual):
        return total_of_pieces(back_partial(residual), OBS)

    def squared_norm(gradient):
        return taken_together(jnp.sum(gradient * gradient, axis=0), PATCH)

    slip = jnp.zeros((col_count, epochs), jnp.float32)
    reg_resid = jnp.zeros((col_count, epochs), jnp.float32)
    gradient = gradient_of(residual)
    grad_norm = squared_norm(gradient)
    direction = gradient
    for iteration in range(ITERS):
        image = summed_on_arrival(
            jnp.dot(green, direction, precision=highest, preferred_element_type=jnp.float32),
            PATCH,
            0,
        )
        image, image_sq = (image, jnp.sum(image * image, axis=0))
        extended = extended_2(direction, ((PATCH, 0),), BAND)
        reg_image = reg_weight * (
            4.0 * direction
            - extended[local_ids[0]]
            - extended[local_ids[1]]
            - extended[local_ids[2]]
        )
        reg_sq = jnp.where(obs_first, jnp.sum(reg_image * reg_image, axis=0), 0.0)
        curvature = over_axes_2(image_sq + reg_sq, OBS_PATCH)
        step_size = grad_norm / curvature
        slip = slip + step_size * direction
        if iteration + 1 < ITERS:
            residual = residual - step_size * image
            reg_resid = reg_resid - step_size * reg_image
            spread = jnp.zeros((col_count + 2 * BAND, epochs), jnp.float32)
            for slot in range(3):
                spread = spread.at[local_ids[slot]].add(reg_resid)
            from_left = shifted(spread[BAND + col_count :], PATCH, 1)
            from_right = shifted(spread[:BAND], PATCH, -1)
            filler = jnp.zeros((col_count - BAND, epochs), jnp.float32)
            inside = (
                spread[BAND : BAND + col_count]
                + jnp.concatenate([from_left, filler], 0)
                + jnp.concatenate([filler, from_right], 0)
            )
            gradient = gradient_of(residual) + reg_weight * (4.0 * reg_resid - inside)
            next_norm = squared_norm(gradient)
            direction = gradient + next_norm / grad_norm * direction
            grad_norm = next_norm
    return slip


def solution(mesh):
    split = Mesh(mesh.devices.reshape(4, 4, 16, 2), ("obs_0", "obs_1", "patch_0", "patch_1"))
    in_specs = (P(OBS, PATCH), P(OBS, None), P(None, PATCH), P())
    out_specs = P(PATCH, None)
    return jax.shard_map(
        shards, mesh=split, in_specs=in_specs, out_specs=out_specs, check_vma=False
    )
```

profile of v0, /device:TPU:1, one launch (start us, length us, event | category | flops | bytes accessed | tf_op | source)
XLA Modules:
  0.0 751.9 jit_solution(1936652341242088612)
XLA Ops:
  7.4 30.9 %all-gather = f32[640,128]{1,0:T(8,128)S(1)} all-gather(f32[40,128]{1,0:T(8,128)S(1)} %constant_dynamic-slice_fusion), channel_id=2, replica_groups=mesh['obs_0'=4,'obs_1'=4,'patch_0'=16,'patch_1'=2] {'patch_0'}, dimensions={0}, use_global_device_ids=true | all-gather | bytes 348160 | tf_op jit(solution)/shard_map/all_gather | solution.py:53
  38.3 9.9 %all_gather.37 = f32[32,40,128]{2,1,0:T(8,128)S(1)} all-gather(f32[16,40,128]{2,1,0:T(8,128)S(1)} %bitcast.84), channel_id=1, replica_groups=mesh['obs_0'=4,'obs_1'=4,'patch_0'=16,'patch_1'=2] {'patch_1'}, dimensions={0}, use_global_device_ids=true | all-gather | bytes 983040 | tf_op jit(solution)/shard_map/all_gather | solution.py:53
  51.3 67.2 %all-gather.10.cloned.1.call-done = f32[10240,128]{0,1:T(8,128)} async-done(((f32[640,128]{0,1:T(8,128)}), f32[10240,128]{0,1:T(8,128)}) %all-gather.10.cloned.1.call-update) | async-done | bytes 5242896 | tf_op jit(solution)/shard_map/all_gather | solution.py:65
  118.4 3.4 copy.59
  124.1 13.2 %all-to-all-start = ((f32[32,1,128]{2,1,0:T(1,128)}), f32[32,1,128]{2,1,0:T(1,128)S(1)}, u32[]{:S(2)}, u32[]{:S(2)}) async-start(f32[32,1,128]{2,1,0:T(1,128)} %broadcast_in_dim.21), calls=%async_computation | async-start | bytes 32768 | tf_op jit(solution)/shard_map/all_to_all | solution.py:71
  137.3 5.3 convolution_bitcast_fusion.2
  144.8 4.3 all-to-all-done
  149.1 7.9 %all-to-all-start.1 = ((f32[32,40,128]{2,1,0:T(8,128)}), f32[32,40,128]{2,1,0:T(8,128)}, u32[]{:S(2)}, u32[]{:S(2)}) async-start(f32[32,40,128]{2,1,0:T(8,128)} %bitcast.75), calls=%async_computation.1 | async-start | bytes 1310720 | tf_op jit(solution)/shard_map/all_to_all | solution.py:40
  160.5 3.5 collective-permute-start
  166.0 16.8 %collective-permute-done = f32[128,128]{1,0:T(8,128)S(1)} collective-permute-done((f32[128,128]{1,0:T(8,128)}, f32[128,128]{1,0:T(8,128)S(1)}, u32[]{:S(2)}, u32[]{:S(2)}) %collective-permute-start) | collective-permute-done | bytes 65568 | tf_op jit(solution)/shard_map/ppermute | solution.py:21
  182.8 4.5 collective-permute-done.1
  202.1 8.4 %psum.84 = f32[128]{0:T(128)S(1)} all-reduce(f32[128]{0:T(128)S(1)} %fusion.23), channel_id=1, replica_groups=mesh['obs_0'=4,'obs_1'=4,'patch_0'=16,'patch_1'=2] {'obs_0'}, use_global_device_ids=true, to_apply=%region_6.7 | all-reduce | flops 128 | bytes 1024 | tf_op jit(solution)/shard_map/psum | solution.py:83
  210.5 6.5 psum.85
  217.0 24.1 %psum.86 = f32[128]{0:T(128)S(1)} all-reduce(f32[128]{0:T(128)S(1)} %psum.85), channel_id=1, replica_groups=mesh['obs_0'=4,'obs_1'=4,'patch_0'=16,'patch_1'=2] {'patch_0'}, use_global_device_ids=true, to_apply=%region_8.9 | all-reduce | flops 128 | bytes 1024 | tf_op jit(solution)/shard_map/psum | solution.py:83
  241.2 13.6 %psum.87 = f32[128]{0:T(128)S(1)} all-reduce(f32[128]{0:T(128)S(1)} %psum.86), channel_id=1, replica_groups=mesh['obs_0'=4,'obs_1'=4,'patch_0'=16,'patch_1'=2] {'patch_1'}, use_global_device_ids=true, to_apply=%region_9.10 | all-reduce | flops 128 | bytes 1024 | tf_op jit(solution)/shard_map/psum | solution.py:83
  255.5 21.6 %all-gather.2 = f32[640,128]{1,0:T(8,128)S(1)} all-gather(f32[40,128]{1,0:T(8,128)S(1)} %multiply_subtract_fusion.6), channel_id=4, replica_groups=mesh['obs_0'=4,'obs_1'=4,'patch_0'=16,'patch_1'=2] {'patch_0'}, dimensions={0}, use_global_device_ids=true | all-gather | bytes 348160 | tf_op jit(solution)/shard_map/all_gather | solution.py:53
  277.1 9.2 %all_gather.41 = f32[32,40,128]{2,1,0:T(8,128)S(1)} all-gather(f32[16,40,128]{2,1,0:T(8,128)S(1)} %bitcast.86), channel_id=1, replica_groups=mesh['obs_0'=4,'obs_1'=4,'patch_0'=16,'patch_1'=2] {'patch_1'}, dimensions={0}, use_global_device_ids=true | all-gather | bytes 983040 | tf_op jit(solution)/shard_map/all_gather | solution.py:53
  289.4 7.2 scatter_custom_fusion
  296.6 7.7 %scatter_custom_fusion.1 = f32[896,128]{1,0:T(8,128)} fusion(f32[896,128]{1,0:T(8,128)} %scatter_custom_fusion, s32[640]{0:T(1024)S(1)} %get-tuple-element.7, f32[640,128]{1,0:T(8,128)} %get-tuple-element.15, f32[]{:T(128)} %constant.8.clone.1, f32[128]{0:T(128)S(1)} %div.23), kind=kCustom, calls=%fused_computation.55 | custom fusion | flops 245760 | bytes 787456 | tf_op jit(solution)/shard_map/scatter-add | solution.py:145
  304.3 7.7 %scatter_custom_fusion.2 = f32[896,128]{1,0:T(8,128)} fusion(f32[896,128]{1,0:T(8,128)} %scatter_custom_fusion.1, s32[640]{0:T(1024)S(1)} %get-tuple-element.6, f32[640,128]{1,0:T(8,128)} %get-tuple-element.15, f32[]{:T(128)} %constant.8.clone.1, f32[128]{0:T(128)S(1)} %div.23), kind=kCustom, calls=%fused_computation.54 | custom fusion | flops 245760 | bytes 787456 | tf_op jit(solution)/shard_map/scatter-add | solution.py:145
  318.9 35.8 %all-gather.12.cloned.1.call-done = f32[10240,128]{0,1:T(8,128)} async-done(((f32[640,128]{0,1:T(8,128)}), f32[10240,128]{0,1:T(8,128)}) %all-gather.12.cloned.1.call-update) | async-done | bytes 5242896 | tf_op jit(solution)/shard_map/all_gather | solution.py:65
  363.5 24.8 %all_to_all.33 = f32[32,1,128]{2,1,0:T(1,128)S(1)} all-to-all(f32[32,1,128]{2,1,0:T(1,128)S(1)} %broadcast_in_dim.25), channel_id=1, replica_groups=mesh['obs_0'=4,'obs_1'=4,'patch_0'=16,'patch_1'=2] {'patch_0','patch_1'}, dimensions={0} | all-to-all | bytes 32768 | tf_op jit(solution)/shard_map/all_to_all | solution.py:71
  390.2 4.3 convolution_bitcast_fusion.1
  396.6 5.1 all-to-all-start.3
  402.7 3.5 collective-permute-start.4
  408.2 19.1 %collective-permute-done.4 = f32[128,128]{1,0:T(8,128)S(1)} collective-permute-done((f32[128,128]{1,0:T(8,128)S(1)}, f32[128,128]{1,0:T(8,128)S(1)}, u32[]{:S(2)}, u32[]{:S(2)}) %collective-permute-start.4) | collective-permute-done | bytes 65568 | tf_op jit(solution)/shard_map/ppermute | solution.py:21
  427.3 5.0 collective-permute-done.5
  447.1 8.4 %psum.88 = f32[128]{0:T(128)S(1)} all-reduce(f32[128]{0:T(128)S(1)} %fusion.24), channel_id=1, replica_groups=mesh['obs_0'=4,'obs_1'=4,'patch_0'=16,'patch_1'=2] {'obs_0'}, use_global_device_ids=true, to_apply=%region_19.20 | all-reduce | flops 128 | bytes 1024 | tf_op jit(solution)/shard_map/psum | solution.py:83
  455.5 6.5 psum.89
  462.0 23.9 %psum.90 = f32[128]{0:T(128)S(1)} all-reduce(f32[128]{0:T(128)S(1)} %psum.89), channel_id=1, replica_groups=mesh['obs_0'=4,'obs_1'=4,'patch_0'=16,'patch_1'=2] {'patch_0'}, use_global_device_ids=true, to_apply=%region_21.22 | all-reduce | flops 128 | bytes 1024 | tf_op jit(solution)/shard_map/psum | solution.py:83
  485.9 13.6 %psum.91 = f32[128]{0:T(128)S(1)} all-reduce(f32[128]{0:T(128)S(1)} %psum.90), channel_id=1, replica_groups=mesh['obs_0'=4,'obs_1'=4,'patch_0'=16,'patch_1'=2] {'patch_1'}, use_global_device_ids=true, to_apply=%region_22.23 | all-reduce | flops 128 | bytes 1024 | tf_op jit(solution)/shard_map/psum | solution.py:83
  499.5 21.6 %all-gather.4 = f32[640,128]{1,0:T(8,128)S(1)} all-gather(f32[40,128]{1,0:T(8,128)S(1)} %multiply_subtract_fusion.5), channel_id=6, replica_groups=mesh['obs_0'=4,'obs_1'=4,'patch_0'=16,'patch_1'=2] {'patch_0'}, dimensions={0}, use_global_device_ids=true | all-gather | bytes 348160 | tf_op jit(solution)/shard_map/all_gather | solution.py:53
  521.1 9.3 %all_gather.45 = f32[32,40,128]{2,1,0:T(8,128)S(1)} all-gather(f32[16,40,128]{2,1,0:T(8,128)S(1)} %bitcast.85), channel_id=1, replica_groups=mesh['obs_0'=4,'obs_1'=4,'patch_0'=16,'patch_1'=2] {'patch_1'}, dimensions={0}, use_global_device_ids=true | all-gather | bytes 983040 | tf_op jit(solution)/shard_map/all_gather | solution.py:53
  535.3 7.2 scatter_custom_fusion.3
  542.5 7.6 %scatter_fusion = f32[896,128]{1,0:T(8,128)} fusion(f32[896,128]{1,0:T(8,128)} %scatter_custom_fusion.3, s32[640]{0:T(1024)S(1)} %get-tuple-element.7, f32[640,128]{1,0:T(8,128)} %multiply_subtract_fusion), kind=kCustom, calls=%fused_computation.13 | custom fusion | flops 81920 | bytes 985600 | tf_op jit(solution)/shard_map/scatter-add | solution.py:145
  550.1 7.6 %scatter_fusion.1 = f32[896,128]{1,0:T(8,128)} fusion(f32[896,128]{1,0:T(8,128)} %scatter_fusion, s32[640]{0:T(1024)S(1)} %get-tuple-element.6, f32[640,128]{1,0:T(8,128)} %multiply_subtract_fusion), kind=kCustom, calls=%fused_computation.14 | custom fusion | flops 81920 | bytes 985600 | tf_op jit(solution)/shard_map/scatter-add | solution.py:145
  564.8 33.9 %all-gather.14.cloned.1.call-done = f32[10240,128]{0,1:T(8,128)} async-done(((f32[640,128]{0,1:T(8,128)}), f32[10240,128]{0,1:T(8,128)}) %all-gather.14.cloned.1.call-update) | async-done | bytes 5242896 | tf_op jit(solution)/shard_map/all_gather | solution.py:65
  598.7 3.4 copy.61
  607.6 24.8 %all_to_all.34 = f32[32,1,128]{2,1,0:T(1,128)S(1)} all-to-all(f32[32,1,128]{2,1,0:T(1,128)S(1)} %broadcast_in_dim.27), channel_id=1, replica_groups=mesh['obs_0'=4,'obs_1'=4,'patch_0'=16,'patch_1'=2] {'patch_0','patch_1'}, dimensions={0} | all-to-all | bytes 32768 | tf_op jit(solution)/shard_map/all_to_all | solution.py:71
  634.2 4.3 convolution_bitcast_fusion
  640.7 5.1 all-to-all-start.5
  646.7 3.5 collective-permute-start.8
  652.2 19.2 %collective-permute-done.8 = f32[128,128]{1,0:T(8,128)S(1)} collective-permute-done((f32[128,128]{1,0:T(8,128)S(1)}, f32[128,128]{1,0:T(8,128)S(1)}, u32[]{:S(2)}, u32[]{:S(2)}) %collective-permute-start.8) | collective-permute-done | bytes 65568 | tf_op jit(solution)/shard_map/ppermute | solution.py:21
  671.4 5.0 collective-permute-done.9
  690.5 8.4 %psum.92 = f32[128]{0:T(128)S(1)} all-reduce(f32[128]{0:T(128)S(1)} %fusion.25), channel_id=1, replica_groups=mesh['obs_0'=4,'obs_1'=4,'patch_0'=16,'patch_1'=2] {'obs_0'}, use_global_device_ids=true, to_apply=%region_32.33 | all-reduce | flops 128 | bytes 1024 | tf_op jit(solution)/shard_map/psum | solution.py:83
  698.9 6.8 psum.93
  705.6 23.7 %psum.94 = f32[128]{0:T(128)S(1)} all-reduce(f32[128]{0:T(128)S(1)} %psum.93), channel_id=1, replica_groups=mesh['obs_0'=4,'obs_1'=4,'patch_0'=16,'patch_1'=2] {'patch_0'}, use_global_device_ids=true, to_apply=%region_34.35 | all-reduce | flops 128 | bytes 1024 | tf_op jit(solution)/shard_map/psum | solution.py:83
  729.3 13.6 %psum.95 = f32[128]{0:T(128)S(1)} all-reduce(f32[128]{0:T(128)S(1)} %psum.94), channel_id=1, replica_groups=mesh['obs_0'=4,'obs_1'=4,'patch_0'=16,'patch_1'=2] {'patch_1'}, use_global_device_ids=true, to_apply=%region_35.36 | all-reduce | flops 128 | bytes 1024 | tf_op jit(solution)/shard_map/psum | solution.py:83
  (102 shorter events, 110.2 us)
Async XLA Ops:
  6.5 41.7 %copy-start = (f32[1280,640]{1,0:T(8,128)S(1)}, f32[1280,640]{1,0:T(8,128)}, u32[]{:S(2)}) copy-start(f32[1280,640]{1,0:T(8,128)} %param.4) | copy-start | bytes 9830404
  6.5 111.9 %all-gather.10.cloned.1.call-start = ((), (), s32[]{:S(2)}) async-start(), calls=%async_computation.6 | async-start | bytes 5570560 | tf_op jit(solution)/shard_map/all_gather | solution.py:65
  122.7 0.7 copy-start.3
  124.1 24.9 %all-to-all-start = ((f32[32,1,128]{2,1,0:T(1,128)}), f32[32,1,128]{2,1,0:T(1,128)S(1)}, u32[]{:S(2)}, u32[]{:S(2)}) async-start(f32[32,1,128]{2,1,0:T(1,128)} %broadcast_in_dim.21), calls=%async_computation | async-start | bytes 32768 | tf_op jit(solution)/shard_map/all_to_all | solution.py:71
  137.3 19.7 %copy-start.5 = (s32[3,640]{1,0:T(4,128)S(1)}, s32[3,640]{1,0:T(4,128)}, u32[]{:S(2)}) copy-start(s32[3,640]{1,0:T(4,128)} %param.6) | copy-start | bytes 23044
  149.1 51.8 %all-to-all-start.1 = ((f32[32,40,128]{2,1,0:T(8,128)}), f32[32,40,128]{2,1,0:T(8,128)}, u32[]{:S(2)}, u32[]{:S(2)}) async-start(f32[32,40,128]{2,1,0:T(8,128)} %bitcast.75), calls=%async_computation.1 | async-start | bytes 1310720 | tf_op jit(solution)/shard_map/all_to_all | solution.py:40
  157.0 197.6 %all-gather.12.cloned.1.call-start = ((), (), s32[]{:S(2)}) async-start(), calls=%async_computation.7 | async-start | bytes 5570560 | tf_op jit(solution)/shard_map/all_gather | solution.py:65
  160.5 22.3 %collective-permute-start = (f32[128,128]{1,0:T(8,128)}, f32[128,128]{1,0:T(8,128)S(1)}, u32[]{:S(2)}, u32[]{:S(2)}) collective-permute-start(f32[128,128]{1,0:T(8,128)} %get-tuple-element.24), channel_id=1, source_target_pairs={{0,1},{1,2},{2,3},{3,4},{4,5},{5,6},{6,7},{7,8},{8,9},{9,10},{10,1... | collective-permute-start | bytes 196616 | tf_op jit(solution)/shard_map/ppermute | solution.py:21
  164.1 23.2 %collective-permute-start.1 = (f32[128,128]{1,0:T(8,128)S(1)}, f32[128,128]{1,0:T(8,128)S(1)}, u32[]{:S(2)}, u32[]{:S(2)}) collective-permute-start(f32[128,128]{1,0:T(8,128)S(1)} %get-tuple-element.25), channel_id=1, source_target_pairs={{1,0},{2,1},{3,2},{4,3},{5,4},{6,5},{7,6},{8,7},{9,8},{10,9},{11,1... | collective-permute-start | bytes 196616 | tf_op jit(solution)/shard_map/ppermute | solution.py:22
  192.3 6.5 copy-start.4
  313.4 48.0 %collective-permute-start.2 = (f32[128,128]{1,0:T(8,128)}, f32[128,128]{1,0:T(8,128)S(1)}, u32[]{:S(2)}, u32[]{:S(2)}) collective-permute-start(f32[128,128]{1,0:T(8,128)} %get-tuple-element.18), channel_id=1, source_target_pairs={{0,1},{1,2},{2,3},{3,4},{4,5},{5,6},{6,7},{7,8},{8,9},{9,10},{10,1... | collective-permute-start | bytes 196616 | tf_op jit(solution)/shard_map/ppermute | solution.py:30
  316.7 44.8 %collective-permute-start.3 = (f32[128,128]{1,0:T(8,128)S(1)}, f32[128,128]{1,0:T(8,128)S(1)}, u32[]{:S(2)}, u32[]{:S(2)}) collective-permute-start(f32[128,128]{1,0:T(8,128)S(1)} %get-tuple-element.19), channel_id=1, source_target_pairs={{1,0},{2,1},{3,2},{4,3},{5,4},{6,5},{7,6},{8,7},{9,8},{10,9},{11,1... | collective-permute-start | bytes 196616 | tf_op jit(solution)/shard_map/ppermute | solution.py:30
  389.4 0.7 copy-start.1
  396.6 49.3 %all-to-all-start.3 = ((f32[32,40,128]{2,1,0:T(8,128)}), f32[32,40,128]{2,1,0:T(8,128)}, u32[]{:S(2)}, u32[]{:S(2)}) async-start(f32[32,40,128]{2,1,0:T(8,128)} %bitcast.76), calls=%async_computation.3 | async-start | bytes 1310720 | tf_op jit(solution)/shard_map/all_to_all | solution.py:40
  401.7 197.0 %all-gather.14.cloned.1.call-start = ((), (), s32[]{:S(2)}) async-start(), calls=%async_computation.8 | async-start | bytes 5570560 | tf_op jit(solution)/shard_map/all_gather | solution.py:65
  402.7 24.6 %collective-permute-start.4 = (f32[128,128]{1,0:T(8,128)S(1)}, f32[128,128]{1,0:T(8,128)S(1)}, u32[]{:S(2)}, u32[]{:S(2)}) collective-permute-start(f32[128,128]{1,0:T(8,128)S(1)} %get-tuple-element.22), channel_id=1, source_target_pairs={{0,1},{1,2},{2,3},{3,4},{4,5},{5,6},{6,7},{7,8},{8,9},{9,10},{10,1... | collective-permute-start | bytes 196616 | tf_op jit(solution)/shard_map/ppermute | solution.py:21
  406.2 26.0 %collective-permute-start.5 = (f32[128,128]{1,0:T(8,128)S(1)}, f32[128,128]{1,0:T(8,128)S(1)}, u32[]{:S(2)}, u32[]{:S(2)}) collective-permute-start(f32[128,128]{1,0:T(8,128)S(1)} %get-tuple-element.23), channel_id=1, source_target_pairs={{1,0},{2,1},{3,2},{4,3},{5,4},{6,5},{7,6},{8,7},{9,8},{10,9},{11,1... | collective-permute-start | bytes 196616 | tf_op jit(solution)/shard_map/ppermute | solution.py:22
  559.2 46.3 %collective-permute-start.6 = (f32[128,128]{1,0:T(8,128)}, f32[128,128]{1,0:T(8,128)S(1)}, u32[]{:S(2)}, u32[]{:S(2)}) collective-permute-start(f32[128,128]{1,0:T(8,128)} %get-tuple-element.16), channel_id=1, source_target_pairs={{0,1},{1,2},{2,3},{3,4},{4,5},{5,6},{6,7},{7,8},{8,9},{9,10},{10,1... | collective-permute-start | bytes 196616 | tf_op jit(solution)/shard_map/ppermute | solution.py:30
  562.6 43.0 %collective-permute-start.7 = (f32[128,128]{1,0:T(8,128)S(1)}, f32[128,128]{1,0:T(8,128)S(1)}, u32[]{:S(2)}, u32[]{:S(2)}) collective-permute-start(f32[128,128]{1,0:T(8,128)S(1)} %get-tuple-element.17), channel_id=1, source_target_pairs={{1,0},{2,1},{3,2},{4,3},{5,4},{6,5},{7,6},{8,7},{9,8},{10,9},{11,1... | collective-permute-start | bytes 196616 | tf_op jit(solution)/shard_map/ppermute | solution.py:30
  633.5 0.7 copy-start.2
  640.7 48.6 %all-to-all-start.5 = ((f32[32,40,128]{2,1,0:T(8,128)}), f32[32,40,128]{2,1,0:T(8,128)}, u32[]{:S(2)}, u32[]{:S(2)}) async-start(f32[32,40,128]{2,1,0:T(8,128)} %bitcast.77), calls=%async_computation.5 | async-start | bytes 1310720 | tf_op jit(solution)/shard_map/all_to_all | solution.py:40
  646.7 24.7 %collective-permute-start.8 = (f32[128,128]{1,0:T(8,128)S(1)}, f32[128,128]{1,0:T(8,128)S(1)}, u32[]{:S(2)}, u32[]{:S(2)}) collective-permute-start(f32[128,128]{1,0:T(8,128)S(1)} %get-tuple-element.20), channel_id=1, source_target_pairs={{0,1},{1,2},{2,3},{3,4},{4,5},{5,6},{6,7},{7,8},{8,9},{9,10},{10,1... | collective-permute-start | bytes 196616 | tf_op jit(solution)/shard_map/ppermute | solution.py:21
  650.3 26.1 %collective-permute-start.9 = (f32[128,128]{1,0:T(8,128)S(1)}, f32[128,128]{1,0:T(8,128)S(1)}, u32[]{:S(2)}, u32[]{:S(2)}) collective-permute-start(f32[128,128]{1,0:T(8,128)S(1)} %get-tuple-element.21), channel_id=1, source_target_pairs={{1,0},{2,1},{3,2},{4,3},{5,4},{6,5},{7,6},{8,7},{9,8},{10,9},{11,1... | collective-permute-start | bytes 196616 | tf_op jit(solution)/shard_map/ppermute | solution.py:22
Sparse Core Ops, SparseCore 0:
  51.4 66.9 all-gather.9
  289.5 65.0 all-gather.11
  533.6 65.1 all-gather.13
where the time goes:
time: 762 us; the launch traced here: 752 us
  blocking collectives  309 us (41%)
  waiting for transfers between devices  211 us (28%)
  other arithmetic  74.5 us (10%)
  local copies, waits for them, and re-layouts  61.7 us (8%)
  starting transfers between devices  58.7 us (8%)
  matrix products  22.9 us (3%)
  between operations  13.9 us (2%)
    psum x12, blocking collectives, over_axes_2(): shard = lax.psum(shard, axis)  157 us
    all_gather x3, waiting for transfers between devices, total_of_pieces(): pieces = lax.all_gather(shard, axis)  137 us
    all_gather x6, blocking collectives, all_blocks(): pieces = lax.all_gather(pieces, axes[k], axis=0, tiled=True)  102 us
    ppermute x3, waiting for transfers between devices, extended_2(): before = lax.ppermute(last, axis, up)  55.1 us
    all_to_all x2, blocking collectives, sent_to_all(): lax.all_to_all(jnp.broadcast_to(shard[None], (length, *shard.shape)), axi...  49.6 us
    scatter-add x6, other arithmetic, shards(): spread = spread.at[local_ids[slot]].add(reg_resid)  45 us
    all_to_all x3, starting transfers between devices, summed_on_arrival(): lax.all_to_all(cut_along(shard, dim, length), axis, 0, 0, tiled=True)  18.1 us
  transfers between devices with their start and end apart: 17, of which 10 were waited for; matrix products, arithmetic and copies ran while one was open for 15% of the time, Pallas kernels for 0%

commit v1 on v0

--- a/solution.py
+++ b/solution.py
@@ -50,7 +50,9 @@
 def all_blocks(shard, axes, sequence):
     pieces = shard[None]
     for k in sequence:
-        pieces = lax.all_gather(pieces, axes[k], axis=0, tiled=True)
+        pieces = jnp.concatenate(
+            lax.all_to_all(jnp.stack([pieces] * lax.axis_size(axes[k])), axes[k], 0, 0), axis=0
+        )
     block = [lax.axis_size(axes[k]) for k in reversed(sequence)]
     pieces = pieces.reshape(*block, *shard.shape)
     turned = sorted(range(len(sequence)), key=lambda place: sequence[len(sequence) - 1 - place])

time: 762 us -> 764 us (level)
  blocking collectives: 309 us -> 318 us
    all_to_all x0 -> x6, blocking collectives: none -> 111 us  [all_blocks(): lax.all_to_all(jnp.stack([pieces] * lax.axis_size(axes[k])), axes[k], 0, 0)]
    all_gather x6 -> x0, blocking collectives: 102 us -> none  [all_blocks(): pieces = lax.all_gather(pieces, axes[k], axis=0, tiled=True)]
where the time goes in v1:
time: 764 us; the launch traced here: 753 us
  blocking collectives  318 us (42%)
  waiting for transfers between devices  204 us (27%)
  other arithmetic  74.7 us (10%)
  local copies, waits for them, and re-layouts  61.7 us (8%)
  starting transfers between devices  58.1 us (8%)
  matrix products  22.9 us (3%)
  between operations  13.6 us (2%)
    psum x12, blocking collectives, over_axes_2(): shard = lax.psum(shard, axis)  157 us
    all_gather x3, waiting for transfers between devices, total_of_pieces(): pieces = lax.all_gather(shard, axis)  130 us
    all_to_all x6, blocking collectives, all_blocks(): lax.all_to_all(jnp.stack([pieces] * lax.axis_size(axes[k])), axes[k], 0, 0)  111 us
    ppermute x3, waiting for transfers between devices, extended_2(): before = lax.ppermute(last, axis, up)  55.1 us
    all_to_all x2, blocking collectives, sent_to_all(): lax.all_to_all(jnp.broadcast_to(shard[None], (length, *shard.shape)), axi...  49.6 us
    scatter-add x6, other arithmetic, shards(): spread = spread.at[local_ids[slot]].add(reg_resid)  45.1 us
    all_to_all x3, starting transfers between devices, summed_on_arrival(): lax.all_to_all(cut_along(shard, dim, length), axis, 0, 0, tiled=True)  18.1 us
  transfers between devices with their start and end apart: 17, of which 10 were waited for; matrix products, arithmetic and copies ran while one was open for 15% of the time, Pallas kernels for 0%

profile of v1, /device:TPU:1, one launch (start us, length us, event | category | flops | bytes accessed | tf_op | source)
XLA Modules:
  0.0 753.3 jit_solution(1170588523259111757)
XLA Ops:
  7.4 31.0 %all_to_all.63 = f32[16,1,40,128]{3,2,1,0:T(8,128)S(1)} all-to-all(f32[16,1,40,128]{3,2,1,0:T(8,128)S(1)} %stack.18), channel_id=1, replica_groups=mesh['obs_0'=4,'obs_1'=4,'patch_0'=16,'patch_1'=2] {'patch_0'}, dimensions={0} | all-to-all | bytes 655360 | tf_op jit(solution)/shard_map/all_to_all | solution.py:54
  38.5 10.4 %all_to_all.64 = f32[2,16,40,128]{3,2,1,0:T(8,128)S(1)} all-to-all(f32[2,16,40,128]{3,2,1,0:T(8,128)S(1)} %pad_maximum_fusion), channel_id=1, replica_groups=mesh['obs_0'=4,'obs_1'=4,'patch_0'=16,'patch_1'=2] {'patch_1'}, dimensions={0} | all-to-all | bytes 1310720 | tf_op jit(solution)/shard_map/all_to_all | solution.py:54
  52.0 66.5 %all-gather.7.cloned.1.call-done = f32[10240,128]{0,1:T(8,128)} async-done(((f32[640,128]{0,1:T(8,128)}), f32[10240,128]{0,1:T(8,128)}) %all-gather.7.cloned.1.call-update) | async-done | bytes 5242896 | tf_op jit(solution)/shard_map/all_gather | solution.py:67
  118.4 3.4 copy.53
  124.2 13.2 %all-to-all-start.2 = ((f32[32,1,128]{2,1,0:T(1,128)}), f32[32,1,128]{2,1,0:T(1,128)S(1)}, u32[]{:S(2)}, u32[]{:S(2)}) async-start(f32[32,1,128]{2,1,0:T(1,128)} %broadcast_in_dim.14), calls=%async_computation.2 | async-start | bytes 32768 | tf_op jit(solution)/shard_map/all_to_all | solution.py:73
  137.4 5.3 convolution_bitcast_fusion.2
  144.8 4.3 all-to-all-done.2
  149.1 7.9 %all-to-all-start.3 = ((f32[32,40,128]{2,1,0:T(8,128)}), f32[32,40,128]{2,1,0:T(8,128)}, u32[]{:S(2)}, u32[]{:S(2)}) async-start(f32[32,40,128]{2,1,0:T(8,128)} %bitcast.72), calls=%async_computation.3 | async-start | bytes 1310720 | tf_op jit(solution)/shard_map/all_to_all | solution.py:40
  160.6 3.5 collective-permute-start
  166.0 16.8 %collective-permute-done = f32[128,128]{1,0:T(8,128)S(1)} collective-permute-done((f32[128,128]{1,0:T(8,128)}, f32[128,128]{1,0:T(8,128)S(1)}, u32[]{:S(2)}, u32[]{:S(2)}) %collective-permute-start) | collective-permute-done | bytes 65568 | tf_op jit(solution)/shard_map/ppermute | solution.py:21
  182.8 4.5 collective-permute-done.1
  202.1 8.4 %psum.84 = f32[128]{0:T(128)S(1)} all-reduce(f32[128]{0:T(128)S(1)} %fusion.23), channel_id=1, replica_groups=mesh['obs_0'=4,'obs_1'=4,'patch_0'=16,'patch_1'=2] {'obs_0'}, use_global_device_ids=true, to_apply=%region_6.7 | all-reduce | flops 128 | bytes 1024 | tf_op jit(solution)/shard_map/psum | solution.py:85
  210.5 6.5 psum.85
  217.1 24.1 %psum.86 = f32[128]{0:T(128)S(1)} all-reduce(f32[128]{0:T(128)S(1)} %psum.85), channel_id=1, replica_groups=mesh['obs_0'=4,'obs_1'=4,'patch_0'=16,'patch_1'=2] {'patch_0'}, use_global_device_ids=true, to_apply=%region_8.9 | all-reduce | flops 128 | bytes 1024 | tf_op jit(solution)/shard_map/psum | solution.py:85
  241.2 13.6 %psum.87 = f32[128]{0:T(128)S(1)} all-reduce(f32[128]{0:T(128)S(1)} %psum.86), channel_id=1, replica_groups=mesh['obs_0'=4,'obs_1'=4,'patch_0'=16,'patch_1'=2] {'patch_1'}, use_global_device_ids=true, to_apply=%region_9.10 | all-reduce | flops 128 | bytes 1024 | tf_op jit(solution)/shard_map/psum | solution.py:85
  255.5 24.2 %all_to_all.65 = f32[16,1,40,128]{3,2,1,0:T(8,128)S(1)} all-to-all(f32[16,1,40,128]{3,2,1,0:T(8,128)S(1)} %stack.20), channel_id=1, replica_groups=mesh['obs_0'=4,'obs_1'=4,'patch_0'=16,'patch_1'=2] {'patch_0'}, dimensions={0} | all-to-all | bytes 655360 | tf_op jit(solution)/shard_map/all_to_all | solution.py:54
  279.8 10.6 %all_to_all.66 = f32[2,16,40,128]{3,2,1,0:T(8,128)S(1)} all-to-all(f32[2,16,40,128]{3,2,1,0:T(8,128)S(1)} %pad_maximum_fusion.1), channel_id=1, replica_groups=mesh['obs_0'=4,'obs_1'=4,'patch_0'=16,'patch_1'=2] {'patch_1'}, dimensions={0} | all-to-all | bytes 1310720 | tf_op jit(solution)/shard_map/all_to_all | solution.py:54
  293.4 7.2 scatter_custom_fusion
  300.7 7.7 %scatter_custom_fusion.1 = f32[896,128]{1,0:T(8,128)} fusion(f32[896,128]{1,0:T(8,128)} %scatter_custom_fusion, s32[640]{0:T(1024)S(1)} %get-tuple-element.7, f32[640,128]{1,0:T(8,128)} %get-tuple-element.15, f32[]{:T(128)} %constant.8.clone.1, f32[128]{0:T(128)S(1)} %div.23), kind=kCustom, calls=%fused_computation.58 | custom fusion | flops 245760 | bytes 787456 | tf_op jit(solution)/shard_map/scatter-add | solution.py:147
  308.4 7.7 %scatter_custom_fusion.2 = f32[896,128]{1,0:T(8,128)} fusion(f32[896,128]{1,0:T(8,128)} %scatter_custom_fusion.1, s32[640]{0:T(1024)S(1)} %get-tuple-element.6, f32[640,128]{1,0:T(8,128)} %get-tuple-element.15, f32[]{:T(128)} %constant.8.clone.1, f32[128]{0:T(128)S(1)} %div.23), kind=kCustom, calls=%fused_computation.57 | custom fusion | flops 245760 | bytes 787456 | tf_op jit(solution)/shard_map/scatter-add | solution.py:147
  322.6 33.0 %all-gather.9.cloned.1.call-done = f32[10240,128]{0,1:T(8,128)} async-done(((f32[640,128]{0,1:T(8,128)}), f32[10240,128]{0,1:T(8,128)}) %all-gather.9.cloned.1.call-update) | async-done | bytes 5242896 | tf_op jit(solution)/shard_map/all_gather | solution.py:67
  355.5 3.4 copy.54
  364.4 24.8 %all_to_all.67 = f32[32,1,128]{2,1,0:T(1,128)S(1)} all-to-all(f32[32,1,128]{2,1,0:T(1,128)S(1)} %broadcast_in_dim.17), channel_id=1, replica_groups=mesh['obs_0'=4,'obs_1'=4,'patch_0'=16,'patch_1'=2] {'patch_0','patch_1'}, dimensions={0} | all-to-all | bytes 32768 | tf_op jit(solution)/shard_map/all_to_all | solution.py:73
  391.1 4.3 convolution_bitcast_fusion.1
  397.5 5.1 all-to-all-start.7
  403.6 3.5 collective-permute-start.4
  409.1 19.1 %collective-permute-done.4 = f32[128,128]{1,0:T(8,128)S(1)} collective-permute-done((f32[128,128]{1,0:T(8,128)S(1)}, f32[128,128]{1,0:T(8,128)S(1)}, u32[]{:S(2)}, u32[]{:S(2)}) %collective-permute-start.4) | collective-permute-done | bytes 65568 | tf_op jit(solution)/shard_map/ppermute | solution.py:21
  428.2 5.0 collective-permute-done.5
  448.0 8.4 %psum.88 = f32[128]{0:T(128)S(1)} all-reduce(f32[128]{0:T(128)S(1)} %fusion.24), channel_id=1, replica_groups=mesh['obs_0'=4,'obs_1'=4,'patch_0'=16,'patch_1'=2] {'obs_0'}, use_global_device_ids=true, to_apply=%region_19.20 | all-reduce | flops 128 | bytes 1024 | tf_op jit(solution)/shard_map/psum | solution.py:85
  456.4 6.5 psum.89
  463.0 23.9 %psum.90 = f32[128]{0:T(128)S(1)} all-reduce(f32[128]{0:T(128)S(1)} %psum.89), channel_id=1, replica_groups=mesh['obs_0'=4,'obs_1'=4,'patch_0'=16,'patch_1'=2] {'patch_0'}, use_global_device_ids=true, to_apply=%region_21.22 | all-reduce | flops 128 | bytes 1024 | tf_op jit(solution)/shard_map/psum | solution.py:85
  486.8 13.6 %psum.91 = f32[128]{0:T(128)S(1)} all-reduce(f32[128]{0:T(128)S(1)} %psum.90), channel_id=1, replica_groups=mesh['obs_0'=4,'obs_1'=4,'patch_0'=16,'patch_1'=2] {'patch_1'}, use_global_device_ids=true, to_apply=%region_22.23 | all-reduce | flops 128 | bytes 1024 | tf_op jit(solution)/shard_map/psum | solution.py:85
  500.5 24.2 %all_to_all.68 = f32[16,1,40,128]{3,2,1,0:T(8,128)S(1)} all-to-all(f32[16,1,40,128]{3,2,1,0:T(8,128)S(1)} %stack.22), channel_id=1, replica_groups=mesh['obs_0'=4,'obs_1'=4,'patch_0'=16,'patch_1'=2] {'patch_0'}, dimensions={0} | all-to-all | bytes 655360 | tf_op jit(solution)/shard_map/all_to_all | solution.py:54
  524.7 10.6 %all_to_all.69 = f32[2,16,40,128]{3,2,1,0:T(8,128)S(1)} all-to-all(f32[2,16,40,128]{3,2,1,0:T(8,128)S(1)} %pad_maximum_fusion.2), channel_id=1, replica_groups=mesh['obs_0'=4,'obs_1'=4,'patch_0'=16,'patch_1'=2] {'patch_1'}, dimensions={0} | all-to-all | bytes 1310720 | tf_op jit(solution)/shard_map/all_to_all | solution.py:54
  540.3 7.2 scatter_custom_fusion.3
  547.5 7.7 %scatter_fusion = f32[896,128]{1,0:T(8,128)} fusion(f32[896,128]{1,0:T(8,128)} %scatter_custom_fusion.3, s32[640]{0:T(1024)S(1)} %get-tuple-element.7, f32[640,128]{1,0:T(8,128)} %multiply_subtract_fusion), kind=kCustom, calls=%fused_computation.13 | custom fusion | flops 81920 | bytes 985600 | tf_op jit(solution)/shard_map/scatter-add | solution.py:147
  555.2 7.6 %scatter_fusion.1 = f32[896,128]{1,0:T(8,128)} fusion(f32[896,128]{1,0:T(8,128)} %scatter_fusion, s32[640]{0:T(1024)S(1)} %get-tuple-element.6, f32[640,128]{1,0:T(8,128)} %multiply_subtract_fusion), kind=kCustom, calls=%fused_computation.14 | custom fusion | flops 81920 | bytes 985600 | tf_op jit(solution)/shard_map/scatter-add | solution.py:147
  569.6 31.0 %all-gather.11.cloned.1.call-done = f32[10240,128]{0,1:T(8,128)} async-done(((f32[640,128]{0,1:T(8,128)}), f32[10240,128]{0,1:T(8,128)}) %all-gather.11.cloned.1.call-update) | async-done | bytes 5242896 | tf_op jit(solution)/shard_map/all_gather | solution.py:67
  609.4 24.8 %all_to_all.70 = f32[32,1,128]{2,1,0:T(1,128)S(1)} all-to-all(f32[32,1,128]{2,1,0:T(1,128)S(1)} %broadcast_in_dim.18), channel_id=1, replica_groups=mesh['obs_0'=4,'obs_1'=4,'patch_0'=16,'patch_1'=2] {'patch_0','patch_1'}, dimensions={0} | all-to-all | bytes 32768 | tf_op jit(solution)/shard_map/all_to_all | solution.py:73
  636.1 4.3 convolution_bitcast_fusion
  642.5 5.1 all-to-all-start.11
  648.5 3.5 collective-permute-start.8
  654.0 19.2 %collective-permute-done.8 = f32[128,128]{1,0:T(8,128)S(1)} collective-permute-done((f32[128,128]{1,0:T(8,128)S(1)}, f32[128,128]{1,0:T(8,128)S(1)}, u32[]{:S(2)}, u32[]{:S(2)}) %collective-permute-start.8) | collective-permute-done | bytes 65568 | tf_op jit(solution)/shard_map/ppermute | solution.py:21
  673.2 5.0 collective-permute-done.9
  692.3 8.4 %psum.92 = f32[128]{0:T(128)S(1)} all-reduce(f32[128]{0:T(128)S(1)} %fusion.25), channel_id=1, replica_groups=mesh['obs_0'=4,'obs_1'=4,'patch_0'=16,'patch_1'=2] {'obs_0'}, use_global_device_ids=true, to_apply=%region_32.33 | all-reduce | flops 128 | bytes 1024 | tf_op jit(solution)/shard_map/psum | solution.py:85
  700.7 6.8 psum.93
  707.5 23.7 %psum.94 = f32[128]{0:T(128)S(1)} all-reduce(f32[128]{0:T(128)S(1)} %psum.93), channel_id=1, replica_groups=mesh['obs_0'=4,'obs_1'=4,'patch_0'=16,'patch_1'=2] {'patch_0'}, use_global_device_ids=true, to_apply=%region_34.35 | all-reduce | flops 128 | bytes 1024 | tf_op jit(solution)/shard_map/psum | solution.py:85
  731.1 13.6 %psum.95 = f32[128]{0:T(128)S(1)} all-reduce(f32[128]{0:T(128)S(1)} %psum.94), channel_id=1, replica_groups=mesh['obs_0'=4,'obs_1'=4,'patch_0'=16,'patch_1'=2] {'patch_1'}, use_global_device_ids=true, to_apply=%region_35.36 | all-reduce | flops 128 | bytes 1024 | tf_op jit(solution)/shard_map/psum | solution.py:85
  (108 shorter events, 109.8 us)
Async XLA Ops:
  6.5 42.4 %copy-start = (f32[1280,640]{1,0:T(8,128)S(1)}, f32[1280,640]{1,0:T(8,128)}, u32[]{:S(2)}) copy-start(f32[1280,640]{1,0:T(8,128)} %param.4) | copy-start | bytes 9830404
  6.5 111.9 %all-gather.7.cloned.1.call-start = ((), (), s32[]{:S(2)}) async-start(), calls=%async_computation.12 | async-start | bytes 5570560 | tf_op jit(solution)/shard_map/all_gather | solution.py:67
  122.7 0.7 copy-start.3
  124.2 24.9 %all-to-all-start.2 = ((f32[32,1,128]{2,1,0:T(1,128)}), f32[32,1,128]{2,1,0:T(1,128)S(1)}, u32[]{:S(2)}, u32[]{:S(2)}) async-start(f32[32,1,128]{2,1,0:T(1,128)} %broadcast_in_dim.14), calls=%async_computation.2 | async-start | bytes 32768 | tf_op jit(solution)/shard_map/all_to_all | solution.py:73
  137.4 19.7 %copy-start.5 = (s32[3,640]{1,0:T(4,128)S(1)}, s32[3,640]{1,0:T(4,128)}, u32[]{:S(2)}) copy-start(s32[3,640]{1,0:T(4,128)} %param.6) | copy-start | bytes 23044
  149.1 51.8 %all-to-all-start.3 = ((f32[32,40,128]{2,1,0:T(8,128)}), f32[32,40,128]{2,1,0:T(8,128)}, u32[]{:S(2)}, u32[]{:S(2)}) async-start(f32[32,40,128]{2,1,0:T(8,128)} %bitcast.72), calls=%async_computation.3 | async-start | bytes 1310720 | tf_op jit(solution)/shard_map/all_to_all | solution.py:40
  157.0 198.5 %all-gather.9.cloned.1.call-start = ((), (), s32[]{:S(2)}) async-start(), calls=%async_computation.13 | async-start | bytes 5570560 | tf_op jit(solution)/shard_map/all_gather | solution.py:67
  160.6 22.3 %collective-permute-start = (f32[128,128]{1,0:T(8,128)}, f32[128,128]{1,0:T(8,128)S(1)}, u32[]{:S(2)}, u32[]{:S(2)}) collective-permute-start(f32[128,128]{1,0:T(8,128)} %get-tuple-element.24), channel_id=1, source_target_pairs={{0,1},{1,2},{2,3},{3,4},{4,5},{5,6},{6,7},{7,8},{8,9},{9,10},{10,1... | collective-permute-start | bytes 196616 | tf_op jit(solution)/shard_map/ppermute | solution.py:21
  164.1 23.2 %collective-permute-start.1 = (f32[128,128]{1,0:T(8,128)S(1)}, f32[128,128]{1,0:T(8,128)S(1)}, u32[]{:S(2)}, u32[]{:S(2)}) collective-permute-start(f32[128,128]{1,0:T(8,128)S(1)} %get-tuple-element.25), channel_id=1, source_target_pairs={{1,0},{2,1},{3,2},{4,3},{5,4},{6,5},{7,6},{8,7},{9,8},{10,9},{11,1... | collective-permute-start | bytes 196616 | tf_op jit(solution)/shard_map/ppermute | solution.py:22
  192.3 6.5 copy-start.4
  317.5 44.9 %collective-permute-start.2 = (f32[128,128]{1,0:T(8,128)}, f32[128,128]{1,0:T(8,128)S(1)}, u32[]{:S(2)}, u32[]{:S(2)}) collective-permute-start(f32[128,128]{1,0:T(8,128)} %get-tuple-element.18), channel_id=1, source_target_pairs={{0,1},{1,2},{2,3},{3,4},{4,5},{5,6},{6,7},{7,8},{8,9},{9,10},{10,1... | collective-permute-start | bytes 196616 | tf_op jit(solution)/shard_map/ppermute | solution.py:30
  320.5 41.9 %collective-permute-start.3 = (f32[128,128]{1,0:T(8,128)S(1)}, f32[128,128]{1,0:T(8,128)S(1)}, u32[]{:S(2)}, u32[]{:S(2)}) collective-permute-start(f32[128,128]{1,0:T(8,128)S(1)} %get-tuple-element.19), channel_id=1, source_target_pairs={{1,0},{2,1},{3,2},{4,3},{5,4},{6,5},{7,6},{8,7},{9,8},{10,9},{11,1... | collective-permute-start | bytes 196616 | tf_op jit(solution)/shard_map/ppermute | solution.py:30
  390.3 0.7 copy-start.1
  397.5 49.3 %all-to-all-start.7 = ((f32[32,40,128]{2,1,0:T(8,128)}), f32[32,40,128]{2,1,0:T(8,128)}, u32[]{:S(2)}, u32[]{:S(2)}) async-start(f32[32,40,128]{2,1,0:T(8,128)} %bitcast.73), calls=%async_computation.7 | async-start | bytes 1310720 | tf_op jit(solution)/shard_map/all_to_all | solution.py:40
  402.7 197.9 %all-gather.11.cloned.1.call-start = ((), (), s32[]{:S(2)}) async-start(), calls=%async_computation.14 | async-start | bytes 5570560 | tf_op jit(solution)/shard_map/all_gather | solution.py:67
  403.6 24.6 %collective-permute-start.4 = (f32[128,128]{1,0:T(8,128)S(1)}, f32[128,128]{1,0:T(8,128)S(1)}, u32[]{:S(2)}, u32[]{:S(2)}) collective-permute-start(f32[128,128]{1,0:T(8,128)S(1)} %get-tuple-element.22), channel_id=1, source_target_pairs={{0,1},{1,2},{2,3},{3,4},{4,5},{5,6},{6,7},{7,8},{8,9},{9,10},{10,1... | collective-permute-start | bytes 196616 | tf_op jit(solution)/shard_map/ppermute | solution.py:21
  407.1 26.0 %collective-permute-start.5 = (f32[128,128]{1,0:T(8,128)S(1)}, f32[128,128]{1,0:T(8,128)S(1)}, u32[]{:S(2)}, u32[]{:S(2)}) collective-permute-start(f32[128,128]{1,0:T(8,128)S(1)} %get-tuple-element.23), channel_id=1, source_target_pairs={{1,0},{2,1},{3,2},{4,3},{5,4},{6,5},{7,6},{8,7},{9,8},{10,9},{11,1... | collective-permute-start | bytes 196616 | tf_op jit(solution)/shard_map/ppermute | solution.py:22
  564.3 43.1 %collective-permute-start.6 = (f32[128,128]{1,0:T(8,128)}, f32[128,128]{1,0:T(8,128)S(1)}, u32[]{:S(2)}, u32[]{:S(2)}) collective-permute-start(f32[128,128]{1,0:T(8,128)} %get-tuple-element.16), channel_id=1, source_target_pairs={{0,1},{1,2},{2,3},{3,4},{4,5},{5,6},{6,7},{7,8},{8,9},{9,10},{10,1... | collective-permute-start | bytes 196616 | tf_op jit(solution)/shard_map/ppermute | solution.py:30
  567.2 40.2 %collective-permute-start.7 = (f32[128,128]{1,0:T(8,128)S(1)}, f32[128,128]{1,0:T(8,128)S(1)}, u32[]{:S(2)}, u32[]{:S(2)}) collective-permute-start(f32[128,128]{1,0:T(8,128)S(1)} %get-tuple-element.17), channel_id=1, source_target_pairs={{1,0},{2,1},{3,2},{4,3},{5,4},{6,5},{7,6},{8,7},{9,8},{10,9},{11,1... | collective-permute-start | bytes 196616 | tf_op jit(solution)/shard_map/ppermute | solution.py:30
  635.3 0.7 copy-start.2
  642.5 48.6 %all-to-all-start.11 = ((f32[32,40,128]{2,1,0:T(8,128)}), f32[32,40,128]{2,1,0:T(8,128)}, u32[]{:S(2)}, u32[]{:S(2)}) async-start(f32[32,40,128]{2,1,0:T(8,128)} %bitcast.74), calls=%async_computation.11 | async-start | bytes 1310720 | tf_op jit(solution)/shard_map/all_to_all | solution.py:40
  648.5 24.7 %collective-permute-start.8 = (f32[128,128]{1,0:T(8,128)S(1)}, f32[128,128]{1,0:T(8,128)S(1)}, u32[]{:S(2)}, u32[]{:S(2)}) collective-permute-start(f32[128,128]{1,0:T(8,128)S(1)} %get-tuple-element.20), channel_id=1, source_target_pairs={{0,1},{1,2},{2,3},{3,4},{4,5},{5,6},{6,7},{7,8},{8,9},{9,10},{10,1... | collective-permute-start | bytes 196616 | tf_op jit(solution)/shard_map/ppermute | solution.py:21
  652.1 26.1 %collective-permute-start.9 = (f32[128,128]{1,0:T(8,128)S(1)}, f32[128,128]{1,0:T(8,128)S(1)}, u32[]{:S(2)}, u32[]{:S(2)}) collective-permute-start(f32[128,128]{1,0:T(8,128)S(1)} %get-tuple-element.21), channel_id=1, source_target_pairs={{1,0},{2,1},{3,2},{4,3},{5,4},{6,5},{7,6},{8,7},{9,8},{10,9},{11,1... | collective-permute-start | bytes 196616 | tf_op jit(solution)/shard_map/ppermute | solution.py:22
Sparse Core Ops, SparseCore 0:
  52.1 66.3 all-gather.6
  293.6 61.9 all-gather.8
  538.6 61.9 all-gather.10
